TPU v7x, 32 devices: a whole 2x2x4 slice. The times are simulated.
32 devices in a mesh: blk: 4 (over y, x), half: 2 (over core), rep: 4 (over z).
Axes of the slice: x: 2, y: 2, z: 4, core: 2. Of those that a mesh axis runs over, the one named last changes fastest.
Arguments:
- tokens: bfloat16 [1024, 2048], P('blk'), may hold values from -6 to 6
- experts: int32 [1024, 6], P('blk'), may hold values from 0 to 63, all different within a row; in each aligned block of 256 rows (0 to 255, 256 to 511, ...) at most 32 rows name the same one
- gates: bfloat16 [1024, 6], P('blk'), may hold values from 0.099609375 to 1
- w_gate: bfloat16 [64, 1408, 2048], P('blk', ('half', 'rep')), may hold values from -0.125 to 0.125
- w_up: bfloat16 [64, 1408, 2048], P('blk', ('half', 'rep')), may hold values from -0.125 to 0.125
- w_down: bfloat16 [64, 1408, 2048], P('blk', ('half', 'rep')), may hold values from -0.15625 to 0.15625
- shared_gate: bfloat16 [1408, 2048], P(('half', 'rep')), may hold values from -0.125 to 0.125
- shared_up: bfloat16 [1408, 2048], P(('half', 'rep')), may hold values from -0.125 to 0.125
- shared_down: bfloat16 [1408, 2048], P(('half', 'rep')), may hold values from -0.15625 to 0.15625
Outputs:
- mixed: bfloat16 [1024, 2048], P('blk', ('half', 'rep'))
Inputs may be any that keep to these rules, and one draw needn't show every extreme that they name: Each row names 6 different experts. Among the 256 rows held by one index of blk no expert is named by more than 32 rows, a bound that some block reaches.
All inputs are finite; a program needn't handle non-finite values.
Results may differ from a plain program's by a relative error of at most 0.0055.
Values may be sent and summed in bfloat16 or wider, within the bound.
No kernel may reach another device: no remote copies, remote signals or barrier semaphores. Data moves between devices by JAX's collectives and lax.ppermute only.
A program may use at most 128 MiB of HBM per device.

v0:
```python
import jax
import jax.numpy as jnp
from jax import lax
from jax.sharding import PartitionSpec as P

E = 64
CAP = 32


def hidden_units(token_rows, gate_matrix, up_weight):
    gate_values = jnp.einsum(
        "kan,ktn->kat", token_rows, gate_matrix, preferred_element_type=jnp.float32
    )
    raised_rows = jnp.einsum(
        "kan,ktn->kat", token_rows, up_weight, preferred_element_type=jnp.float32
    )
    return (jax.nn.silu(gate_values) * raised_rows).astype(jnp.bfloat16)


def place_slots(flat, ranks, block_size, which, slot_count):
    inside = ranks // block_size == which
    local = jnp.where(inside, flat * block_size + ranks % block_size, -1)
    return local[:, None] == jnp.arange(slot_count, dtype=jnp.int32)[None, :]


def per_device(tokens, experts, gates, w_gate, w_up, w_down, shared_gate, shared_up, shared_down):
    token_count = tokens.shape[0]
    width = tokens.shape[1]
    topk = experts.shape[1]
    exp_local = w_gate.shape[0]
    blk_count = lax.axis_size("blk")
    slot_block = CAP // lax.axis_size("rep")
    member_rep = lax.axis_index("rep")
    flat = experts.reshape(-1)
    onehot = (flat[:, None] == jnp.arange(E, dtype=jnp.int32)[None, :]).astype(jnp.int32)
    before = jnp.cumsum(onehot, axis=0) - onehot
    ranks = jnp.sum(before * onehot, axis=1)
    placing = place_slots(flat, ranks, slot_block, member_rep, E * slot_block).reshape(
        token_count, topk, -1
    )
    weighting = jnp.sum(
        placing.astype(jnp.float32) * gates.astype(jnp.float32)[:, :, None], axis=1
    ).astype(jnp.bfloat16)
    selector = jnp.any(placing, axis=1).astype(jnp.bfloat16)
    filled = jnp.einsum("ts,td->sd", selector, tokens, preferred_element_type=jnp.float32).astype(
        jnp.bfloat16
    )
    filled = filled.reshape(E, 1, slot_block, width)
    arrived = lax.all_to_all(filled, "blk", split_axis=0, concat_axis=1, tiled=True)
    token_rows = arrived.reshape(exp_local, -1, width)
    every_hidden = hidden_units(lax.all_gather(token_rows, "rep", axis=1, tiled=True), w_gate, w_up)
    mine = lax.all_to_all(every_hidden, "rep", split_axis=1, concat_axis=2, tiled=True)
    partial_value = jnp.einsum(
        "otv,ovj->otj",
        mine,
        lax.all_gather(w_down, "rep", axis=1, tiled=True),
        preferred_element_type=jnp.float32,
    )
    block_out = partial_value.astype(jnp.bfloat16).reshape(exp_local, blk_count, slot_block, width)
    returned = lax.all_to_all(block_out, "blk", split_axis=1, concat_axis=0, tiled=True)
    returned = returned.reshape(E * slot_block, width)
    routed = jnp.dot(weighting, returned, preferred_element_type=jnp.float32)
    shared_hidden = (
        jax.nn.silu(
            jnp.einsum("td,sd->ts", tokens, shared_gate, preferred_element_type=jnp.float32)
        )
        * jnp.einsum("td,sd->ts", tokens, shared_up, preferred_element_type=jnp.float32)
    ).astype(jnp.bfloat16)
    shared_output = jnp.dot(shared_hidden, shared_down, preferred_element_type=jnp.float32)
    routed_share = lax.psum_scatter(routed, ("half", "rep"), scatter_dimension=1, tiled=True)
    shared_share = lax.psum_scatter(shared_output, ("half", "rep"), scatter_dimension=1, tiled=True)
    total = routed_share + shared_share
    return total.astype(jnp.bfloat16)


def solution(mesh):
    return jax.shard_map(
        per_device,
        mesh=mesh,
        in_specs=(
            P("blk", None),
            P("blk", None),
            P("blk", None),
            P("blk", ("half", "rep"), None),
            P("blk", ("half", "rep"), None),
            P("blk", ("half", "rep"), None),
            P(("half", "rep"), None),
            P(("half", "rep"), None),
            P(("half", "rep"), None),
        ),
        out_specs=P("blk", ("half", "rep")),
        check_vma=False,
    )
```

profile of v0, /device:TPU:1, one launch (start us, length us, event | category | flops | bytes accessed | tf_op | source)
XLA Modules:
  0.0 1109.0 jit_solution(772665334566259263)
XLA Ops:
  6.5 0.0 copy-start
  6.5 0.0 copy-start.2
  6.5 0.0 all-gather.3.cloned.1.call-start
  6.5 0.9 copy.61
  7.5 0.1 eq.55
  7.6 0.1 eq.51
  7.8 18.1 %reduce-window.6 = s32[64,12,128]{2,1,0:T(8,128)S(1)} reduce-window(s32[64,12,128]{2,1,0:T(8,128)S(1)} %fusion.6, s32[]{:T(128)} %constant.39.clone.1), window={size=1x1x128 pad=0_0x0_0x127_0}, to_apply=%region_0.0 | reduce-window | flops 12484608 | bytes 786436 | tf_op jit(solution)/shard_map/reduce-window
  25.9 0.2 slice.8
  26.2 0.3 copy.63
  26.5 0.1 copy.64
  26.5 0.2 broadcast_add_fusion
  26.8 0.2 fusion.9
  26.9 0.1 reduce_sum.21
  27.1 0.1 copy.65
  27.2 0.0 copy-done.2
  27.2 0.4 fusion
  27.6 0.0 copy-done
  27.6 0.8 fusion.1
  28.4 28.2 %all_to_all.48 = bf16[64,1,8,2048]{3,2,1,0:T(8,128)(2,1)S(1)} all-to-all(bf16[64,1,8,2048]{3,2,1,0:T(8,128)(2,1)S(1)} %fusion.1), channel_id=1, replica_groups=mesh['blk'=4,'half'=2,'rep'=4] {'blk'}, dimensions={0} | all-to-all | bytes 4194304 | tf_op jit(solution)/shard_map/all_to_all | solution.py:49
  56.6 1.4 copy.79
  58.1 0.0 all-gather.3.cloned.1.call-update
  58.1 0.0 all-gather.5.cloned.1.call-start
  58.1 0.7 all-gather.5.cloned.1.call-update
  58.8 150.4 %all-gather.3.cloned.1.call-done = bf16[16,128,2048]{2,1,0:T(8,128)(2,1)} async-done(((bf16[16,32,2048]{2,1,0:T(8,128)(2,1)}), bf16[16,128,2048]{2,1,0:T(8,128)(2,1)}) %all-gather.3.cloned.1.call-update) | async-done | bytes 8388624 | tf_op jit(solution)/shard_map/all_gather | solution.py:51
  209.2 9.9 fusion.23
  219.1 15.4 %fusion.3 = bf16[16,128,176]{1,2,0:T(8,128)(2,1)S(1)} fusion(bf16[16,128,2048]{2,1,0:T(8,128)(2,1)} %all-gather.3.cloned.1.call-done, bf16[16,176,2048]{2,1,0:T(8,128)(2,1)} %param.13, f32[16,128,176]{1,2,0:T(8,128)S(1)} %fusion.23), kind=kOutput, calls=%fused_computation.10 | convolution fusion | flops 1478557696 | bytes 22085632 | tf_op jit(solution)/shard_map/kan,ktn->kat/dot_general | solution.py:14
  234.5 0.9 copy.71
  235.4 65.3 %all_to_all.49 = bf16[16,128,176]{2,0,1:T(8,128)(2,1)S(1)} all-to-all(bf16[16,128,176]{2,0,1:T(8,128)(2,1)S(1)} %copy.71), channel_id=1, replica_groups=mesh['blk'=4,'half'=2,'rep'=4] {'rep'}, dimensions={1} | all-to-all | bytes 1441792 | tf_op jit(solution)/shard_map/all_to_all | solution.py:52
  300.7 0.8 copy.73
  301.6 1.8 all_to_all.41
  303.3 696.3 %all-gather.5.cloned.1.call-done = bf16[16,704,2048]{2,1,0:T(8,128)(2,1)} async-done(((bf16[16,176,2048]{2,1,0:T(8,128)(2,1)}), bf16[16,704,2048]{2,1,0:T(8,128)(2,1)}) %all-gather.5.cloned.1.call-update) | async-done | bytes 46137360 | tf_op jit(solution)/shard_map/all_gather | solution.py:56
  999.6 18.6 %fusion.2 = bf16[16,4,8,2048]{3,2,1,0:T(8,128)(2,1)S(1)} fusion(bf16[16,32,704]{2,1,0:T(8,128)(2,1)} %all_to_all.41, bf16[16,704,2048]{2,1,0:T(8,128)(2,1)} %all-gather.5.cloned.1.call-done), kind=kOutput, calls=%fused_computation.6 | convolution fusion | flops 1477443584 | bytes 48955392 | tf_op jit(solution)/shard_map/otv,ovj->otj/dot_general | solution.py:53
  1018.3 1.4 copy.74
  1019.7 0.0 copy-start.3
  1019.7 0.0 copy-start.1
  1019.7 4.6 all-to-all-start.2
  1024.3 0.0 reduce-scatter.2.cloned.1.call-start
  1024.3 0.0 copy-done.3
  1024.4 0.6 select_reduce_fusion
  1025.0 0.0 copy-done.1
  1025.0 1.2 fusion.24
  1026.2 2.9 fusion.5
  1029.0 19.7 %all-to-all-done.2 = bf16[16,4,8,2048]{3,2,0,1:T(8,128)(2,1)} async-done(((bf16[16,4,8,2048]{3,2,0,1:T(8,128)(2,1)}), bf16[16,4,8,2048]{3,2,0,1:T(8,128)(2,1)}, u32[]{:S(2)}, u32[]{:S(2)}) %all-to-all-start.2) | async-done | bytes 2097184 | tf_op jit(solution)/shard_map/all_to_all | solution.py:60
  1048.7 3.6 convolution_add_fusion
  1052.3 0.0 reduce-scatter.2.cloned.1.call-update
  1052.4 48.5 %reduce-scatter.2.cloned.1.call-done = f32[256,256]{1,0:T(8,128)} async-done(((f32[256,2048]{1,0:T(8,128)}), f32[256,256]{1,0:T(8,128)}) %reduce-scatter.2.cloned.1.call-update) | async-done | bytes 262160 | tf_op jit(solution)/shard_map/reduce_scatter | solution.py:70
  1100.9 1.6 convert_element_type.38
  (4 shorter events, 0.1 us)
Async XLA Ops:
  6.5 21.1 %copy-start = (bf16[256,2048]{1,0:T(8,128)(2,1)S(1)}, bf16[256,2048]{1,0:T(8,128)(2,1)}, u32[]{:S(2)}) copy-start(bf16[256,2048]{1,0:T(8,128)(2,1)} %param.9) | copy-start | bytes 3145732
  6.5 20.6 %copy-start.2 = (s32[256,6]{0,1:T(8,128)S(1)}, s32[256,6]{0,1:T(8,128)}, u32[]{:S(2)}) copy-start(s32[256,6]{0,1:T(8,128)} %param.10) | copy-start | bytes 18436
  6.5 202.7 %all-gather.3.cloned.1.call-start = ((), (), s32[]{:S(2)}) async-start(), calls=%async_computation.4 | async-start | bytes 10485760 | tf_op jit(solution)/shard_map/all_gather | solution.py:51
  58.1 941.5 %all-gather.5.cloned.1.call-start = ((), (), s32[]{:S(2)}) async-start(), calls=%async_computation.5 | async-start | bytes 57671680 | tf_op jit(solution)/shard_map/all_gather | solution.py:56
  1019.7 4.6 copy-start.3
  1019.7 5.3 copy-start.1
  1019.7 29.0 %all-to-all-start.2 = ((bf16[16,4,8,2048]{3,2,0,1:T(8,128)(2,1)}), bf16[16,4,8,2048]{3,2,0,1:T(8,128)(2,1)}, u32[]{:S(2)}, u32[]{:S(2)}) async-start(bf16[16,4,8,2048]{3,2,0,1:T(8,128)(2,1)} %copy.74), calls=%async_computation.2 | async-start | bytes 4194304 | tf_op jit(solution)/shard_map/all_to_all | solution.py:60
  1024.3 76.6 %reduce-scatter.2.cloned.1.call-start = ((), (), s32[]{:S(2)}) async-start(), calls=%async_computation.6 | async-start | bytes 2359296 | tf_op jit(solution)/shard_map/reduce_scatter | solution.py:70
Sparse Core Ops, SparseCore 0:
  58.2 150.9 all-gather.2
  210.8 788.7 all-gather.4
  1052.5 48.3 reduce-scatter.1
where the time goes:
time: 1110 us
  waiting for transfers between devices  916 us (83%)
  blocking collectives  93.6 us (8%)
  matrix products  52.3 us (5%)
  other arithmetic  21.3 us (2%)
  between operations  13.3 us (1%)
    all_gather x1, waiting for transfers between devices, per_device(): lax.all_gather(w_down, 'rep', axis=1, tiled=True)  696 us
    all_gather x1, waiting for transfers between devices, per_device(): lax.all_gather(token_rows, 'rep', axis=1, tiled=True)  150 us
    all_to_all x1, blocking collectives, per_device(): lax.all_to_all(every_hidden, 'rep', split_axis=1, concat_axis=2, tiled=True)  65.3 us
    reduce_scatter x1, waiting for transfers between devices, per_device(): lax.psum_scatter(routed, ('half', 'rep'), scatter_dimension=1, tiled=True)  48.5 us
    all_to_all x1, blocking collectives, per_device(): lax.all_to_all(filled, 'blk', split_axis=0, concat_axis=1, tiled=True)  28.2 us
  transfers between devices with their start and end apart: 4, of which 4 were waited for; matrix products, arithmetic and copies ran while one was open for 3% of the time, Pallas kernels for 0%

commit v1 on v0

--- a/solution.py
+++ b/solution.py
@@ -5,6 +5,18 @@
 
 E = 64
 CAP = 32
+
+
+def ring_product(x, axis, dim, term):
+    size, mine = (lax.axis_size(axis), lax.axis_index(axis))
+    left = [(i, (i - 1) % size) for i in range(size)]
+    extent = x.shape[dim]
+    current = x
+    total = term(current, mine * extent)
+    for lap in range(1, size):
+        current = lax.ppermute(current, axis, left)
+        total = total + term(current, (mine + lap) % size * extent)
+    return total
 
 
 def hidden_units(token_rows, gate_matrix, up_weight):
@@ -50,11 +62,16 @@
     token_rows = arrived.reshape(exp_local, -1, width)
     every_hidden = hidden_units(lax.all_gather(token_rows, "rep", axis=1, tiled=True), w_gate, w_up)
     mine = lax.all_to_all(every_hidden, "rep", split_axis=1, concat_axis=2, tiled=True)
-    partial_value = jnp.einsum(
-        "otv,ovj->otj",
-        mine,
-        lax.all_gather(w_down, "rep", axis=1, tiled=True),
-        preferred_element_type=jnp.float32,
+    partial_value = ring_product(
+        w_down,
+        "rep",
+        1,
+        lambda own_block, at: jnp.einsum(
+            "otv,ovj->otj",
+            lax.dynamic_slice_in_dim(mine, at, own_block.shape[1], axis=2),
+            own_block,
+            preferred_element_type=jnp.float32,
+        ),
     )
     block_out = partial_value.astype(jnp.bfloat16).reshape(exp_local, blk_count, slot_block, width)
     returned = lax.all_to_all(block_out, "blk", split_axis=1, concat_axis=0, tiled=True)

time: 1110 us -> 1040 us (0.937)
  blocking collectives: 93.6 us -> 26.2 us
  waiting for transfers between devices: 916 us -> 895 us
  starting transfers between devices: 4.66 us -> 20.3 us
    all_gather x1 -> x0, waiting for transfers between devices: 696 us -> none  [per_device(): lax.all_gather(w_down, 'rep', axis=1, tiled=True)]
    ppermute x0 -> x3, waiting for transfers between devices: none -> 578 us  [ring_product(): current = lax.ppermute(current, axis, left)]
    all_to_all x0 -> x1, waiting for transfers between devices: none -> 241 us  [per_device(): lax.all_to_all(every_hidden, 'rep', split_axis=1, concat_axis=2, tiled=True)]
    all_gather x1, waiting for transfers between devices: 150 us -> 0.01 us  [per_device(): lax.all_gather(token_rows, 'rep', axis=1, tiled=True)]
    all_to_all x1 -> x0, blocking collectives: 65.3 us -> none  [per_device(): lax.all_to_all(every_hidden, 'rep', split_axis=1, concat_axis=2, tiled=True)]
    ppermute x0 -> x3, starting transfers between devices: none -> 12.1 us  [ring_product(): current = lax.ppermute(current, axis, left)]
    dot_general x1 -> x4, matrix products: 18.6 us -> 27 us  [per_device(): jnp.einsum('otv,ovj->otj', lax.dynamic_slice_in_dim(mine, at, own_block.s...]
  transfers between devices with their start and end apart: 4 -> 7, of which waited for: 4 -> 5; matrix products, arithmetic and copies ran while one was open for 3% -> 7% of each run, Pallas kernels for 0% -> 0%
where the time goes in v1:
time: 1040 us
  waiting for transfers between devices  895 us (86%)
  matrix products  55.1 us (5%)
  blocking collectives  26.2 us (3%)
  other arithmetic  21.3 us (2%)
  starting transfers between devices  20.3 us (2%)
  between operations  13.6 us (1%)
  local copies, waits for them, and re-layouts  10.4 us (1%)
    ppermute x3, waiting for transfers between devices, ring_product(): current = lax.ppermute(current, axis, left)  578 us
    all_to_all x1, waiting for transfers between devices, per_device(): lax.all_to_all(every_hidden, 'rep', split_axis=1, concat_axis=2, tiled=True)  241 us
    reduce_scatter x1, waiting for transfers between devices, per_device(): lax.psum_scatter(routed, ('half', 'rep'), scatter_dimension=1, tiled=True)  55.8 us
    dot_general x4, matrix products, per_device(): jnp.einsum('otv,ovj->otj', lax.dynamic_slice_in_dim(mine, at, own_block.s...  27 us
    all_to_all x1, blocking collectives, per_device(): lax.all_to_all(filled, 'blk', split_axis=0, concat_axis=1, tiled=True)  26.2 us
  transfers between devices with their start and end apart: 7, of which 5 were waited for; matrix products, arithmetic and copies ran while one was open for 7% of the time, Pallas kernels for 0%

profile of v1, /device:TPU:1, one launch (start us, length us, event | category | flops | bytes accessed | tf_op | source)
XLA Modules:
  0.0 1041.8 jit_solution(6342032153191266410)
XLA Ops:
  6.5 0.0 copy-start
  6.5 4.1 collective-permute-start
  10.7 246.9 %collective-permute-done = bf16[16,176,2048]{2,1,0:T(8,128)(2,1)} collective-permute-done((bf16[16,176,2048]{2,1,0:T(8,128)(2,1)}, bf16[16,176,2048]{2,1,0:T(8,128)(2,1)}, u32[]{:S(2)}, u32[]{:S(2)}) %collective-permute-start) | collective-permute-done | bytes 11534368 | tf_op jit(solution)/shard_map/ppermute | solution.py:17
  257.5 4.0 collective-permute-start.1
  261.5 0.8 copy.61
  262.4 0.1 eq.59
  262.5 0.1 eq.55
  262.7 18.1 %reduce-window.6 = s32[64,12,128]{2,1,0:T(8,128)S(1)} reduce-window(s32[64,12,128]{2,1,0:T(8,128)S(1)} %fusion.6, s32[]{:T(128)} %constant.62.clone.1), window={size=1x1x128 pad=0_0x0_0x127_0}, to_apply=%region_0.0 | reduce-window | flops 12484608 | bytes 786436 | tf_op jit(solution)/shard_map/reduce-window
  280.8 0.2 slice.8
  281.1 0.3 copy.63
  281.4 0.1 copy.64
  281.5 0.2 broadcast_add_fusion
  281.7 0.2 fusion.9
  281.9 0.1 reduce_sum.21
  282.0 0.1 copy.65
  282.1 0.4 fusion
  282.6 0.8 fusion.1
  283.3 26.2 %all_to_all.48 = bf16[64,1,8,2048]{3,2,1,0:T(8,128)(2,1)S(1)} all-to-all(bf16[64,1,8,2048]{3,2,1,0:T(8,128)(2,1)S(1)} %fusion.1), channel_id=1, replica_groups=mesh['blk'=4,'half'=2,'rep'=4] {'blk'}, dimensions={0} | all-to-all | bytes 4194304 | tf_op jit(solution)/shard_map/all_to_all | solution.py:61
  309.5 1.5 copy.79
  311.0 0.0 all-gather.2.cloned.1.call-update
  311.0 331.4 %collective-permute-done.1 = bf16[16,176,2048]{2,1,0:T(8,128)(2,1)} collective-permute-done((bf16[16,176,2048]{2,1,0:T(8,128)(2,1)}, bf16[16,176,2048]{2,1,0:T(8,128)(2,1)}, u32[]{:S(2)}, u32[]{:S(2)}) %collective-permute-start.1) | collective-permute-done | bytes 11534368 | tf_op jit(solution)/shard_map/ppermute | solution.py:17
  642.4 4.0 collective-permute-start.2
  646.4 9.8 fusion.34
  656.2 9.8 fusion.3
  666.1 1.7 copy.71
  667.7 3.7 all-to-all-start.1
  671.5 241.0 %all-to-all-done.1 = bf16[16,128,176]{2,0,1:T(8,128)(2,1)S(1)} async-done(((bf16[16,128,176]{2,0,1:T(8,128)(2,1)}), bf16[16,128,176]{2,0,1:T(8,128)(2,1)S(1)}, u32[]{:S(2)}, u32[]{:S(2)}) %all-to-all-start.1) | async-done | bytes 720928 | tf_op jit(solution)/shard_map/all_to_all | solution.py:64
  912.5 1.0 copy-done.1
  913.5 2.0 copy.73
  915.5 0.9 all_to_all.41
  916.5 6.7 fusion.15
  923.1 6.7 fusion.13
  929.8 6.7 fusion.11
  936.4 0.0 collective-permute-done.2
  936.4 7.1 fusion.2
  943.5 0.0 copy-start.4
  943.5 0.0 copy-start.2
  943.6 1.4 copy.74
  945.0 4.4 all-to-all-start.2
  949.4 0.0 reduce-scatter.2.cloned.1.call-start
  949.5 0.6 select_reduce_fusion
  950.2 1.2 fusion.35
  951.3 2.9 fusion.5
  954.2 19.7 %all-to-all-done.2 = bf16[16,4,8,2048]{3,2,0,1:T(8,128)(2,1)} async-done(((bf16[16,4,8,2048]{3,2,0,1:T(8,128)(2,1)}), bf16[16,4,8,2048]{3,2,0,1:T(8,128)(2,1)}, u32[]{:S(2)}, u32[]{:S(2)}) %all-to-all-start.2) | async-done | bytes 2097184 | tf_op jit(solution)/shard_map/all_to_all | solution.py:77
  973.9 3.6 convolution_add_fusion
  977.5 0.0 reduce-scatter.2.cloned.1.call-update
  977.5 55.8 %reduce-scatter.2.cloned.1.call-done = f32[256,256]{1,0:T(8,128)} async-done(((f32[256,2048]{1,0:T(8,128)}), f32[256,256]{1,0:T(8,128)}) %reduce-scatter.2.cloned.1.call-update) | async-done | bytes 262160 | tf_op jit(solution)/shard_map/reduce_scatter | solution.py:87
  1033.3 1.6 convert_element_type.38
  (12 shorter events, 0.1 us)
Async XLA Ops:
  6.5 276.0 %copy-start = (bf16[256,2048]{1,0:T(8,128)(2,1)S(1)}, bf16[256,2048]{1,0:T(8,128)(2,1)}, u32[]{:S(2)}) copy-start(bf16[256,2048]{1,0:T(8,128)(2,1)} %param.9) | copy-start | bytes 3145732
  6.5 275.5 %copy-start.3 = (s32[256,6]{0,1:T(8,128)S(1)}, s32[256,6]{0,1:T(8,128)}, u32[]{:S(2)}) copy-start(s32[256,6]{0,1:T(8,128)} %param.10) | copy-start | bytes 18436
  6.5 639.9 %all-gather.2.cloned.1.call-start = ((), (), s32[]{:S(2)}) async-start(), calls=%async_computation.4 | async-start | bytes 10485760 | tf_op jit(solution)/shard_map/all_gather | solution.py:63
  6.5 251.0 %collective-permute-start = (bf16[16,176,2048]{2,1,0:T(8,128)(2,1)}, bf16[16,176,2048]{2,1,0:T(8,128)(2,1)}, u32[]{:S(2)}, u32[]{:S(2)}) collective-permute-start(bf16[16,176,2048]{2,1,0:T(8,128)(2,1)} %param.14), channel_id=1, source_target_pairs={{0,3},{1,0},{2,1},{3,2},{4,7},{5,4},{6,5},{7,6},{8,11},{9,8},{10,9... | collective-permute-start | bytes 34603016 | tf_op jit(solution)/shard_map/ppermute | solution.py:17
  257.5 384.9 %collective-permute-start.1 = (bf16[16,176,2048]{2,1,0:T(8,128)(2,1)}, bf16[16,176,2048]{2,1,0:T(8,128)(2,1)}, u32[]{:S(2)}, u32[]{:S(2)}) collective-permute-start(bf16[16,176,2048]{2,1,0:T(8,128)(2,1)} %collective-permute-done), channel_id=1, source_target_pairs={{0,3},{1,0},{2,1},{3,2},{4,7},{5,4},{6,5},{7,6},{8,11},{9,8},{10,9... | collective-permute-start | bytes 34603016 | tf_op jit(solution)/shard_map/ppermute | solution.py:17
  642.4 294.0 %collective-permute-start.2 = (bf16[16,176,2048]{2,1,0:T(8,128)(2,1)}, bf16[16,176,2048]{2,1,0:T(8,128)(2,1)}, u32[]{:S(2)}, u32[]{:S(2)}) collective-permute-start(bf16[16,176,2048]{2,1,0:T(8,128)(2,1)} %collective-permute-done.1), channel_id=1, source_target_pairs={{0,3},{1,0},{2,1},{3,2},{4,7},{5,4},{6,5},{7,6},{8,11},{9,8},{10,9... | collective-permute-start | bytes 34603016 | tf_op jit(solution)/shard_map/ppermute | solution.py:17
  667.7 244.8 %all-to-all-start.1 = ((bf16[16,128,176]{2,0,1:T(8,128)(2,1)}), bf16[16,128,176]{2,0,1:T(8,128)(2,1)S(1)}, u32[]{:S(2)}, u32[]{:S(2)}) async-start(bf16[16,128,176]{2,0,1:T(8,128)(2,1)} %copy.71), calls=%async_computation.1 | async-start | bytes 2097152 | tf_op jit(solution)/shard_map/all_to_all | solution.py:64
  912.5 1.0 copy-start.1
  943.5 6.0 copy-start.4
  943.5 6.6 copy-start.2
  945.0 28.9 %all-to-all-start.2 = ((bf16[16,4,8,2048]{3,2,0,1:T(8,128)(2,1)}), bf16[16,4,8,2048]{3,2,0,1:T(8,128)(2,1)}, u32[]{:S(2)}, u32[]{:S(2)}) async-start(bf16[16,4,8,2048]{3,2,0,1:T(8,128)(2,1)} %copy.74), calls=%async_computation.2 | async-start | bytes 4194304 | tf_op jit(solution)/shard_map/all_to_all | solution.py:77
  949.4 83.9 %reduce-scatter.2.cloned.1.call-start = ((), (), s32[]{:S(2)}) async-start(), calls=%async_computation.5 | async-start | bytes 2359296 | tf_op jit(solution)/shard_map/reduce_scatter | solution.py:87
Sparse Core Ops, SparseCore 0:
  311.1 279.3 all-gather.1
  977.6 55.6 reduce-scatter.1
